TPU v7x, 32 devices: a whole 2x2x4 slice. The times are simulated.
32 devices in a mesh: ctx: 16 (over z, y, core), head: 2 (over x).
Axes of the slice: x: 2, y: 2, z: 4, core: 2. Of those that a mesh axis runs over, the one named last changes fastest.
Arguments:
- hidden: bfloat16 [2048, 8192], P('ctx', 'head'), may hold values from -6 to 6
- query: bfloat16 [2048, 8192], P('ctx', 'head'), may hold values from -60 to 60
- fresh_key_value: bfloat16 [2, 2048, 1024], P(None, 'ctx', 'head'), may hold values from -6 to 6
- cached_key_value: bfloat16 [2, 4096, 1024], P(None, 'ctx', 'head'), may hold values from -6 to 6
- positions: int32 [3, 2048], P(None, 'ctx'), may hold values from 0 to 4095
- out_weight: bfloat16 [8192, 8192], P('head', 'ctx'), may hold values from -0.0625 to 0.0625
- norm_gain: float32 [8192], P('head'), may hold values from 0.25 to 1.75
- layer3_key_value_weight: bfloat16 [8192, 2048], P(None, 'head'), may hold values from -0.0625 to 0.0625
- layer3_key_value_bias: float32 [2048], P('head'), may hold values from -3 to 3
- keep_index: int32 [2048], P('ctx'), may hold values from 0 to 127, as said below
- keep_count: int32 [16], P('ctx'), may hold values from 64 to 128, as said below
Outputs:
- layer2_out: bfloat16 [2048, 8192], P('ctx', 'head')
- layer3_packed_key_value: bfloat16 [2048, 2048], P('ctx', 'head')
Inputs may be any that keep to these rules, and one draw needn't show every extreme that they name: `keep_index`: within each block of 128 entries, the first keep_count entries are the kept rows in rising order (all text rows and every second visual row), the rest the dropped rows in rising order. `keep_count`: some block keeps all 128 rows in every draw.
All inputs are finite; a program needn't handle non-finite values.
Results may differ from a plain program's by a relative error of at most 0.012.
Values may be sent and summed in bfloat16 or wider, within the bound.
A program may use at most 192 MiB of HBM per device.

v0:
```python
import functools

import jax
import jax.numpy as jnp
from jax import lax
from jax.experimental import pallas as pl
from jax.experimental.pallas import tpu as pltpu
from jax.sharding import PartitionSpec as P

HEAD_DIMENSION = 128


def tables(positions, head_size):
    half = head_size // 2
    column = jnp.arange(half)
    frequency = jnp.power(jnp.float32(1000000.0), -(2.0 * column.astype(jnp.float32)) / head_size)
    section = (column >= head_size // 8).astype(jnp.int32) + (
        column >= head_size // 8 + 3 * head_size // 16
    ).astype(jnp.int32)
    places = positions.astype(jnp.float32)
    chosen = jnp.where(
        section[None, :] == 0,
        places[0][:, None],
        jnp.where(section[None, :] == 1, places[1][:, None], places[2][:, None]),
    )
    angles = chosen * frequency[None, :]
    return (jnp.cos(angles), jnp.sin(angles))


def apply_rotary(x, cosine_table, sine_table):
    half = x.shape[-1] // 2
    first_half = x[..., :half]
    second_half = x[..., half:]
    cosine_table = cosine_table[:, None, :]
    sine_table = sine_table[:, None, :]
    return jnp.concatenate(
        [
            first_half * cosine_table - second_half * sine_table,
            second_half * cosine_table + first_half * sine_table,
        ],
        axis=-1,
    )


LOG2E = 1.4426950408889634


def attend_kernel(group, causal, last, row_ref, q_ref, k_ref, v_ref, *rest):
    if last:
        m_in, l_in, a_in, out_ref, m_ref, l_ref, a_ref = rest
    else:
        m_out, l_out, a_out, m_ref, l_ref, a_ref = rest
    step = pl.program_id(1)
    head = k_ref.shape[1]
    rows = q_ref.shape[0]
    block = k_ref.shape[0]

    @pl.when(step == 0)
    def _():
        if last:
            m_ref[...] = m_in[0]
            l_ref[...] = l_in[0]
            a_ref[...] = a_in[0]
        else:
            m_ref[...] = jnp.full_like(m_ref, -1e30)
            l_ref[...] = jnp.zeros_like(l_ref)
            a_ref[...] = jnp.zeros_like(a_ref)

    def update(masked):
        key = k_ref[...]
        value = v_ref[...]
        scale = LOG2E * head ** (-0.5)
        if masked:
            key_pos = step * block + lax.broadcasted_iota(jnp.int32, (rows, block), 1)
            query_pos = row_ref[0] + lax.broadcasted_iota(jnp.int32, (rows, block), 0)
            visible = key_pos <= query_pos
        for g in range(group):
            part = pl.ds(g * rows, rows)
            s = lax.dot_general(
                q_ref[:, g * head : (g + 1) * head],
                key,
                (((1,), (1,)), ((), ())),
                preferred_element_type=jnp.float32,
            )
            if masked:
                s = jnp.where(visible, s, -1e30)
            old = m_ref[part, :]
            new = jnp.maximum(old, jnp.max(s, axis=1, keepdims=True))
            m_ref[part, :] = new
            e = jnp.exp2((s - new[:, :1]) * scale)
            factor = jnp.exp2((old - new) * scale)
            l_ref[part, :] = l_ref[part, :] * factor + jnp.sum(e, axis=1, keepdims=True)
            a_ref[part, :] = a_ref[part, :] * factor + jnp.dot(
                e.astype(jnp.bfloat16), value, preferred_element_type=jnp.float32
            )

    if causal:
        start = step * block

        @pl.when(start + block - 1 <= row_ref[0])
        def _():
            update(False)

        @pl.when((start + block - 1 > row_ref[0]) & (start <= row_ref[0] + rows - 1))
        def _():
            update(True)
    else:
        update(False)

    @pl.when(step == pl.num_programs(1) - 1)
    def _():
        if last:
            for g in range(group):
                part = pl.ds(g * rows, rows)
                out_ref[:, g * head : (g + 1) * head] = (
                    a_ref[part, :] / l_ref[part, :]
                ).astype(out_ref.dtype)
        else:
            m_out[0] = m_ref[...]
            l_out[0] = l_ref[...]
            a_out[0] = a_ref[...]


def attend(query, key_value, first_row, state, head_size):
    rows, width = query.shape
    length = key_value.shape[1]
    kv_local = key_value.shape[2] // head_size
    group = width // head_size // kv_local
    block = 1024
    while length % block:
        block //= 2
    last = state is not None
    high = group * rows
    carry = pl.BlockSpec((1, high, head_size), lambda k, i, r: (k, 0, 0))
    carry_shape = jax.ShapeDtypeStruct((kv_local, high, head_size), jnp.float32)
    wide = pl.BlockSpec((rows, group * head_size), lambda k, i, r: (0, k))
    in_specs = [
        wide,
        pl.BlockSpec((None, block, head_size), lambda k, i, r: (0, i, k)),
        pl.BlockSpec((None, block, head_size), lambda k, i, r: (1, i, k)),
    ] + ([carry] * 3 if last else [])
    operands = (query, key_value, key_value) + (state if last else ())
    return pl.pallas_call(
        functools.partial(attend_kernel, group, last, last),
        out_shape=jax.ShapeDtypeStruct((rows, width), jnp.bfloat16) if last else (carry_shape,) * 3,
        grid_spec=pltpu.PrefetchScalarGridSpec(
            num_scalar_prefetch=1,
            grid=(kv_local, length // block),
            in_specs=in_specs,
            out_specs=wide if last else (carry,) * 3,
            scratch_shapes=[pltpu.VMEM((high, head_size), jnp.float32)] * 3,
        ),
        compiler_params=pltpu.CompilerParams(vmem_limit_bytes=40 * 1024 * 1024),
        cost_estimate=pl.CostEstimate(
            flops=8 * rows * width * length,
            bytes_accessed=4 * length * kv_local * head_size + 4 * rows * width,
            transcendentals=rows * (width // head_size) * length,
        ),
    )(first_row.reshape(1), *operands)


def scatter_kernel(chips, cores, heads, x_ref, o_ref, send_sem, recv_sem, tile, local_sem):
    me = lax.axis_index("ctx")
    h = lax.axis_index("head")
    chip = me // cores
    core = me % cores
    per = chips // heads
    owner_head = chip // per
    slot = h * per + chip % per
    barrier = pltpu.get_barrier_semaphore()
    for d in range(chips):
        there = lax.rem(chip + d, chips) * cores + core
        for e in range(heads):
            if d or e:
                pl.semaphore_signal(
                    barrier,
                    inc=1,
                    device_id=(there, lax.rem(h + e, heads)),
                    device_id_type=pl.DeviceIdType.MESH,
                )
    pl.semaphore_wait(barrier, chips * heads - 1)

    def copy_to(d):
        p = lax.rem(chip + d, chips)
        return pltpu.make_async_remote_copy(
            src_ref=x_ref.at[p],
            dst_ref=o_ref.at[slot],
            send_sem=send_sem.at[d],
            recv_sem=recv_sem.at[slot],
            device_id=(p * cores + core, owner_head),
            device_id_type=pl.DeviceIdType.MESH,
        )

    def receive(s):
        return pltpu.make_async_remote_copy(
            src_ref=x_ref.at[0],
            dst_ref=o_ref.at[s],
            send_sem=send_sem.at[0],
            recv_sem=recv_sem.at[s],
            device_id=(me, lax.rem(h + 1, heads)),
            device_id_type=pl.DeviceIdType.MESH,
        )

    for d in range(1, chips):
        copy_to(d).start()

    @pl.when(owner_head != h)
    def _():
        copy_to(0).start()

    @pl.when(owner_head == h)
    def _():
        into = pltpu.make_async_copy(x_ref.at[chip], tile, local_sem.at[0])
        into.start()
        into.wait()
        out = pltpu.make_async_copy(tile, o_ref.at[slot], local_sem.at[1])
        out.start()
        out.wait()

    for d in range(1, chips):
        copy_to(d).wait_send()

    @pl.when(owner_head != h)
    def _():
        copy_to(0).wait_send()

    for s in range(chips):

        @pl.when(jnp.logical_or(owner_head != h, slot != s))
        def _():
            receive(s).wait_recv()


def scatter_columns(product, chips, cores, heads):
    block = product.shape[1:]
    moved = pl.pallas_call(
        functools.partial(scatter_kernel, chips, cores, heads),
        out_shape=jax.ShapeDtypeStruct(product.shape, product.dtype),
        in_specs=[pl.BlockSpec(memory_space=pl.ANY)],
        out_specs=pl.BlockSpec(memory_space=pl.ANY),
        scratch_shapes=[
            pltpu.SemaphoreType.DMA((chips,)),
            pltpu.SemaphoreType.DMA((chips,)),
            pltpu.VMEM(block, product.dtype),
            pltpu.SemaphoreType.DMA((2,)),
        ],
        compiler_params=pltpu.CompilerParams(collective_id=0, has_side_effects=True),
    )(product)
    return moved.reshape((heads, chips // heads) + block)


def gather_kernel(depth, cores, x_ref, o_ref, send_sem, recv_sem, tile, local_sem):
    me = lax.axis_index("ctx")
    h = lax.axis_index("head")
    chip = me // cores
    core = me % cores
    ring = chip // 2
    side = chip % 2
    pair = ring * 2 + (1 - side)

    def along(d):
        return lax.rem(ring + d, depth)

    barrier = pltpu.get_barrier_semaphore()
    for d in range(1, depth):
        pl.semaphore_signal(
            barrier,
            inc=1,
            device_id=((along(d) * 2 + side) * cores + core, h),
            device_id_type=pl.DeviceIdType.MESH,
        )
    pl.semaphore_signal(
        barrier, inc=1, device_id=(pair * cores + core, h), device_id_type=pl.DeviceIdType.MESH
    )
    pl.semaphore_wait(barrier, depth)

    def send(source, half, origin, target, kind, d):
        return pltpu.make_async_remote_copy(
            src_ref=source,
            dst_ref=o_ref.at[origin, half],
            send_sem=send_sem.at[kind, d],
            recv_sem=recv_sem.at[half, origin],
            device_id=(target * cores + core, h),
            device_id_type=pl.DeviceIdType.MESH,
        )

    def receive(half, origin):
        send(x_ref.at[half], half, origin, pair, 0, 0).wait_recv()

    sent = [send(x_ref.at[0], 0, chip, pair, 0, 0), send(x_ref.at[1], 1, chip, pair, 1, 0)]
    order = [d for pair_of in zip(range(1, depth), range(depth - 1, 0, -1)) for d in pair_of]
    order = list(dict.fromkeys(order))
    for d in order:
        sent.append(send(x_ref.at[1], 1, chip, along(d) * 2 + side, 2, d))
    for d in order:
        sent.append(send(x_ref.at[0], 0, chip, along(d) * 2 + side, 3, d))
    for copy in sent:
        copy.start()
    into = pltpu.make_async_copy(x_ref, tile, local_sem.at[0])
    into.start()
    into.wait()
    out = pltpu.make_async_copy(tile, o_ref.at[chip], local_sem.at[1])
    out.start()

    receive(0, pair)
    for d in order:
        copy = send(o_ref.at[pair, 0], 0, pair, along(d) * 2 + side, 4, d)
        copy.start()
        sent.append(copy)
    for d in order:
        origin = along(d) * 2 + side
        receive(1, origin)
        copy = send(o_ref.at[origin, 1], 1, origin, pair, 1, d)
        copy.start()
        sent.append(copy)
    for d in range(1, depth):
        receive(0, along(d) * 2 + side)
    receive(1, pair)
    for d in range(1, depth):
        receive(0, along(d) * 2 + 1 - side)
        receive(1, along(d) * 2 + 1 - side)
    for copy in sent:
        copy.wait_send()
    out.wait()


def gather_rows(x, chips, cores):
    rows, width = x.shape
    halves = x.reshape(2, rows // 2, width)
    return pl.pallas_call(
        functools.partial(gather_kernel, chips // 2, cores),
        out_shape=jax.ShapeDtypeStruct((chips,) + halves.shape, x.dtype),
        in_specs=[pl.BlockSpec(memory_space=pl.ANY)],
        out_specs=pl.BlockSpec(memory_space=pl.ANY),
        scratch_shapes=[
            pltpu.SemaphoreType.DMA((5, chips // 2)),
            pltpu.SemaphoreType.DMA((2, chips)),
            pltpu.VMEM(halves.shape, x.dtype),
            pltpu.SemaphoreType.DMA((2,)),
        ],
        compiler_params=pltpu.CompilerParams(collective_id=1, has_side_effects=True),
    )(halves).reshape(chips * rows, width)


def exchange(x, axis_name, size):
    return lax.ppermute(x, axis_name, [(i, i ^ 1) for i in range(size)])


def local(
    contexts,
    heads,
    hidden,
    query,
    fresh_key_value,
    cached_key_value,
    positions,
    out_weight,
    norm_gain,
    layer3_key_value_weight,
    layer3_key_value_bias,
    keep_index,
    keep_count,
):
    new_rows = hidden.shape[0]
    head_size = HEAD_DIMENSION
    kv_local = fresh_key_value.shape[2] // head_size
    q_local = query.shape[1] // head_size
    cores = 2
    chips = contexts // cores
    me = lax.axis_index("ctx")
    core = me % cores
    head = lax.axis_index("head")
    cosine_table, sine_table = tables(positions, head_size)
    rotary_query_rows = apply_rotary(
        query.astype(jnp.float32).reshape(new_rows, q_local, head_size), cosine_table, sine_table
    ).astype(jnp.bfloat16).reshape(new_rows, q_local * head_size)
    rotary_key_rows = apply_rotary(
        fresh_key_value[0].astype(jnp.float32).reshape(new_rows, kv_local, head_size),
        cosine_table,
        sine_table,
    ).astype(jnp.bfloat16)
    recent = jnp.stack(
        [rotary_key_rows.reshape(new_rows, kv_local * head_size), fresh_key_value[1]]
    )
    if heads == 2:
        other_gain = exchange(norm_gain, "head", heads)
        whole_gain = jnp.concatenate(
            [jnp.where(head == 0, norm_gain, other_gain), jnp.where(head == 0, other_gain, norm_gain)]
        )
    else:
        whole_gain = lax.all_gather(norm_gain, "head", axis=0, tiled=True)
    other_weight = exchange(out_weight, "ctx", contexts)
    first_row = me * new_rows
    cached_all = lax.all_gather(cached_key_value, "ctx", axis=1, tiled=True)
    recent_all = lax.all_gather(recent, "ctx", axis=1, tiled=True)
    state = attend(rotary_query_rows, cached_all, first_row, None, head_size)
    attn = attend(rotary_query_rows, recent_all, first_row, tuple(state), head_size)
    outputs = gather_rows(attn, chips, cores)
    own = jnp.dot(outputs, out_weight, preferred_element_type=jnp.float32).astype(jnp.bfloat16)
    other = jnp.dot(outputs, other_weight, preferred_element_type=jnp.float32).astype(jnp.bfloat16)
    product = jnp.concatenate(
        [jnp.where(core == 0, own, other), jnp.where(core == 0, other, own)], axis=1
    ).reshape(chips, new_rows, -1)
    parts = scatter_columns(product, chips, cores, heads)
    head_summed = jnp.sum(parts.astype(jnp.float32), axis=0)
    head_summed = head_summed.transpose(1, 0, 2).reshape(hidden.shape)
    layer2_out = (hidden.astype(jnp.float32) + head_summed).astype(jnp.bfloat16)
    if heads == 2:
        other_out = exchange(layer2_out, "head", heads)
        whole_out = jnp.concatenate(
            [
                jnp.where(head == 0, layer2_out, other_out),
                jnp.where(head == 0, other_out, layer2_out),
            ],
            axis=1,
        )
    else:
        whole_out = lax.all_gather(layer2_out, "head", axis=1, tiled=True)
    widened = whole_out.astype(jnp.float32)
    squares = jnp.sum(widened * widened, axis=1)
    level = lax.rsqrt(squares / widened.shape[1] + 1e-06)[:, None]
    full_rows = (widened * level * whole_gain).astype(jnp.bfloat16)
    full_rows = lax.optimization_barrier(full_rows)
    layer_three_key_value = (
        jnp.dot(full_rows, layer3_key_value_weight, preferred_element_type=jnp.float32)
        + layer3_key_value_bias
    ).reshape(new_rows, kv_local, 2, head_size)
    layer_three_keys = apply_rotary(layer_three_key_value[:, :, 0], cosine_table, sine_table)
    layer_three_key_value = (
        jnp.stack([layer_three_keys, layer_three_key_value[:, :, 1]], axis=2)
        .reshape(new_rows, 2 * kv_local * head_size)
        .astype(jnp.bfloat16)
    )
    selected_rows = jnp.take(layer_three_key_value, keep_index, axis=0)
    block_occupied = jnp.arange(new_rows) < keep_count[0]
    layer3_packed_key_value = jnp.where(
        block_occupied[:, None], selected_rows, jnp.zeros_like(selected_rows)
    )
    return (layer2_out, layer3_packed_key_value)


def solution(mesh):
    placed = (
        P("ctx", "head"),
        P("ctx", "head"),
        P(None, "ctx", "head"),
        P(None, "ctx", "head"),
        P(None, "ctx"),
        P("head", "ctx"),
        P("head"),
        P(None, "head"),
        P("head"),
        P("ctx"),
        P("ctx"),
    )
    return jax.shard_map(
        functools.partial(local, mesh.shape["ctx"], mesh.shape["head"]),
        mesh=mesh,
        in_specs=placed,
        out_specs=(P("ctx", "head"), P("ctx", "head")),
        check_vma=False,
    )
```

profile of v0, /device:TPU:28, one launch (start us, length us, event | category | flops | bytes accessed | tf_op | source)
XLA Modules:
  0.0 462.5 jit_solution(14691008060970776861)
XLA Ops:
  7.2 0.7 all-gather.5.cloned.1.call-update
  8.0 0.7 convert_element_type.89
  8.6 1.0 slice_convert_fusion
  10.7 0.7 pad_maximum_fusion.3
  12.1 0.8 subtract_convert_fusion
  12.9 0.6 pad_maximum_fusion.2
  14.1 1.4 copy.21
  15.5 67.6 %all-gather.5.cloned.1.call-done.k_ref.v_ref = bf16[2,4096,512]{2,1,0:T(8,128)(2,1)} async-done(((bf16[2,256,512]{2,1,0:T(8,128)(2,1)}), bf16[2,4096,512]{2,1,0:T(8,128)(2,1)}) %all-gather.5.cloned.1.call-update) | async-done | bytes 8388624 | tf_op jit(solution)/shard_map/all_gather | solution.py:394
  83.1 58.1 %shard_map.122 = (f32[4,1024,128]{2,1,0:T(8,128)S(1)}, f32[4,1024,128]{2,1,0:T(8,128)S(1)}, f32[4,1024,128]{2,1,0:T(8,128)S(1)}) custom-call(s32[1]{0:T(128)} %bitcast.row_ref, bf16[128,4096]{1,0:T(8,128)(2,1)S(1)} %bitcast.38, bf16[2,4096,512]{2,1,0:T(8,128)(2,1)} %all-gather.5.cloned.1.call-done.k_ref.v_ref, ...), custom_call_target="tpu_custom_call" | custom-call | flops 17179869184 | bytes 10485760 | tf_op jit(solution)/shard_map/pallas_call | solution.py:143
  141.3 1.3 copy-done.2
  142.6 1.3 copy-done.4
  143.9 2.2 copy-done.1
  146.1 1.6 copy-done.3
  147.7 1.6 copy-done.5
  149.3 30.3 %shard_map.123 = bf16[128,4096]{1,0:T(8,128)(2,1)S(1)} custom-call(s32[1]{0:T(128)} %bitcast.row_ref, bf16[128,4096]{1,0:T(8,128)(2,1)S(1)} %bitcast.39, bf16[2,2048,512]{2,1,0:T(8,128)(2,1)S(1)} %copy-done.1, bf16[2,2048,512]{2,1,0:T(8,128)(2,1)S(1)} %copy-done.1, f32[4,1024,128]{2,1,0:T(8,128)S(1)} %get-tuple-element.5.rest_0_, ...), custom_call_target="tpu_custom_call" | custom-call | flops 8589934592 | bytes 6291456 | tf_op jit(solution)/shard_map/pallas_call | solution.py:143
  179.6 1.0 copy-done
  180.6 139.3 %shard_map.124 = bf16[8,2,64,4096]{3,2,1,0:T(8,128)(2,1)} custom-call(bf16[2,64,4096]{2,1,0:T(8,128)(2,1)} %bitcast.37), custom_call_target="tpu_custom_call" | custom-call | tf_op jit(solution)/shard_map/pallas_call | solution.py:330
  319.9 9.2 %convolution_convert_fusion.1 = bf16[1024,512]{0,1:T(8,128)(2,1)S(1)} fusion(bf16[1024,4096]{1,0:T(8,128)(2,1)} %bitcast.41, bf16[4096,512]{1,0:T(8,128)(2,1)} %param.16), kind=kOutput, calls=%fused_computation.15 | convolution fusion | flops 4295491584 | bytes 13631488 | tf_op jit(solution)/shard_map/dot_general | solution.py:399
  329.2 6.7 %broadcast_select_fusion.3 = (bf16[1024,512]{0,1:T(8,128)(2,1)S(1)}, bf16[1024,512]{0,1:T(8,128)(2,1)S(1)}) fusion(bf16[1024,512]{0,1:T(8,128)(2,1)S(1)} %convolution_convert_fusion.1, pred[]{:T(512)S(6)} %eq.34, bf16[1024,4096]{1,0:T(8,128)(2,1)S(1)} %bitcast.42, bf16[4096,512]{1,0:T(8,128)(2,1)} %collective-permute-done), kind=kOutput, calls=%fused_computation.22 | convolution fusion | flops 4296540160 | bytes 15728641 | tf_op jit(solution)/shard_map/dot_general | solution.py:400
  336.1 2.6 copy.22
  338.7 59.4 %shard_map.125 = bf16[8,128,1024]{2,1,0:T(8,128)(2,1)} custom-call(bf16[8,128,1024]{2,1,0:T(8,128)(2,1)} %bitcast.43), custom_call_target="tpu_custom_call" | custom-call | tf_op jit(solution)/shard_map/pallas_call | solution.py:236
  398.0 3.6 convert_reduce_fusion
  401.6 1.9 copy.23
  403.5 1.7 fusion.3
  405.3 2.0 collective-permute-start.2
  408.0 21.7 %collective-permute-done.2 = f32[4096]{0:T(1024)S(1)} collective-permute-done((f32[4096]{0:T(1024)S(1)}, f32[4096]{0:T(1024)S(1)}, u32[]{:S(2)}, u32[]{:S(2)}) %collective-permute-start.2) | collective-permute-done | bytes 16416 | tf_op jit(solution)/shard_map/ppermute | solution.py:346
  429.7 1.3 copy.27
  431.1 1.1 fusion
  432.2 11.2 %fusion.2 = bf16[128,8192]{0,1:T(8,128)(2,1)S(1)} fusion(f32[8192]{0:T(1024)S(1)} %pad_maximum_fusion.6, f32[128]{0:T(128)S(1)} %add_rsqrt_fusion, bf16[128,4096]{0,1:T(8,128)(2,1)S(1)} %get-tuple-element.13, bf16[128,4096]{0,1:T(8,128)(2,1)S(1)} %get-tuple-element.12), kind=kLoop, calls=%fused_computation.5 | loop fusion | flops 7340032 | bytes 4227584 | tf_op jit(solution)/shard_map/convert_element_type | solution.py:422
  443.4 8.3 %convolution_add_fusion = f32[128,1024]{1,0:T(8,128)S(1)} fusion(bf16[128,8192]{0,1:T(8,128)(2,1)S(1)} %fusion.2, bf16[8192,1024]{1,0:T(8,128)(2,1)} %param.18, f32[1024]{0:T(1024)S(1)} %copy-done.10), kind=kOutput, calls=%fused_computation.16 | convolution fusion | flops 2147614720 | bytes 19402752 | tf_op jit(solution)/shard_map/dot_general | solution.py:425
  453.9 0.9 gather_fusion
  454.8 0.8 select_select_fusion
  (55 shorter events, 5.0 us)
Async XLA Ops:
  7.2 4.3 copy-start.7
  7.2 75.9 %all-gather.5.cloned.1.call-start = ((), (), s32[]{:S(2)}) async-start(), calls=%async_computation.1 | async-start | bytes 8912896 | tf_op jit(solution)/shard_map/all_gather | solution.py:394
  7.9 136.0 %all-gather.3.cloned.1.call-start = ((), (), s32[]{:S(2)}) async-start(), calls=%async_computation | async-start | bytes 4456448 | tf_op jit(solution)/shard_map/all_gather | solution.py:395
  11.4 317.7 %collective-permute-start = (bf16[4096,512]{1,0:T(8,128)(2,1)}, bf16[4096,512]{1,0:T(8,128)(2,1)}, u32[]{:S(2)}, u32[]{:S(2)}) collective-permute-start(bf16[4096,512]{1,0:T(8,128)(2,1)} %param.16), channel_id=1, source_target_pairs={{0,2},{2,0},{4,6},{6,4},{8,10},{10,8},{12,14},{14,12},{16,18},{18,... | collective-permute-start | bytes 12582920 | tf_op jit(solution)/shard_map/ppermute | solution.py:346
  12.9 1.2 copy-start.8
  141.3 1.3 copy-start.2
  142.6 1.3 copy-start.4
  143.9 2.2 copy-start.1
  146.1 1.6 copy-start.3
  147.7 1.6 copy-start.5
  179.6 1.0 copy-start
  319.9 9.3 %copy-start.6 = (bf16[8,2,64,4096]{3,2,1,0:T(8,128)(2,1)S(1)}, bf16[8,2,64,4096]{3,2,1,0:T(8,128)(2,1)}, u32[]{:S(2)}) copy-start(bf16[8,2,64,4096]{3,2,1,0:T(8,128)(2,1)} %shard_map.124) | copy-start | bytes 25165828
  403.5 1.8 copy-start.9
  403.5 4.4 copy-start.11
  405.2 25.8 %collective-permute-start.1 = (bf16[128,4096]{0,1:T(8,128)(2,1)S(1)}, bf16[128,4096]{0,1:T(8,128)(2,1)S(1)}, u32[]{:S(2)}, u32[]{:S(2)}) collective-permute-start(bf16[128,4096]{0,1:T(8,128)(2,1)S(1)} %fusion.3), channel_id=1, source_target_pairs={{0,1},{1,0},{2,3},{3,2},{4,5},{5,4},{6,7},{7,6},{8,9},{9,8},{10,11... | collective-permute-start | bytes 3145736 | tf_op jit(solution)/shard_map/ppermute | solution.py:346
  405.3 24.4 %collective-permute-start.2 = (f32[4096]{0:T(1024)S(1)}, f32[4096]{0:T(1024)S(1)}, u32[]{:S(2)}, u32[]{:S(2)}) collective-permute-start(f32[4096]{0:T(1024)S(1)} %copy-done.9), channel_id=1, source_target_pairs={{0,1},{1,0},{2,3},{3,2},{4,5},{5,4},{6,7},{7,6},{8,9},{9,8},{10,11... | collective-permute-start | bytes 49160 | tf_op jit(solution)/shard_map/ppermute | solution.py:346
  432.2 11.2 %copy-start.10 = (f32[1024]{0:T(1024)S(1)}, f32[1024]{0:T(1024)}, u32[]{:S(2)}) copy-start(f32[1024]{0:T(1024)} %param.19) | copy-start | bytes 12292
Sparse Core Ops, SparseCore 0:
  10.2 72.8 all-gather.4
  85.9 48.9 all-gather.2
where the time goes:
time: 463 us; the launch traced here: 462 us
  Pallas kernels  287 us (62%)
  waiting for transfers between devices  90 us (19%)
  matrix products  24.2 us (5%)
  other arithmetic  24.1 us (5%)
  local copies, waits for them, and re-layouts  19.6 us (4%)
  between operations  15.1 us (3%)
    pallas_call x1, Pallas kernels, gather_rows(): pl.pallas_call(functools.partial(gather_kernel, chips // 2, cores), out_s...  139 us
    pallas_call x2, Pallas kernels, attend(): pl.pallas_call(functools.partial(attend_kernel, group, last, last), out_s...  88.5 us
    all_gather x1, waiting for transfers between devices, local(): cached_all = lax.all_gather(cached_key_value, 'ctx', axis=1, tiled=True)  67.6 us
    pallas_call x1, Pallas kernels, scatter_columns(): pl.pallas_call(functools.partial(scatter_kernel, chips, cores, heads), ou...  59.4 us
    ppermute x3, waiting for transfers between devices, exchange(): return lax.ppermute(x, axis_name, [(i, i ^ 1) for i in range(size)])  21.7 us
    unnamed x30, local copies, waits for them, and re-layouts  12.7 us
    convert_element_type x1, other arithmetic, local(): full_rows = (widened * level * whole_gain).astype(jnp.bfloat16)  11.2 us
  transfers between devices with their start and end apart: 5, of which 2 were waited for; matrix products, arithmetic and copies ran while one was open for 4% of the time, Pallas kernels for 49%

commit v1 on v0

--- a/solution.py
+++ b/solution.py
@@ -342,6 +342,538 @@
     )(halves).reshape(chips * rows, width)
 
 
+MESH = pl.DeviceIdType.MESH
+
+
+def fused_kernel(depth, group, heads, key_block, *refs):
+    (cos_ref, sin_ref, q_ref, fresh_ref, cached_ref, w_ref, hidden_ref, out_ref,
+     qrot, qall, frot, kc, kf, s_ref, av, st, wv, acc_ref, cst, crecv,
+     kvs, kvr, kys, kcs, loc, qs, qr, ws, wr, wos, wor, wfs, wfr,
+     xs, xr, us, ds, ys, zr, yr, cs, cr) = refs
+    rows = q_ref.shape[0]
+    head_size = kc.shape[2]
+    half = rows // heads
+    cached_rows = cached_ref.shape[1]
+    chips = depth * 2
+    per = chips // heads
+    me = lax.axis_index("ctx")
+    h = lax.axis_index("head")
+    chip = me // 2
+    c = me % 2
+    z = chip // 2
+    y = chip % 2
+    pair_blocks = group // 2
+    pieces = 4 * depth
+    early = depth
+    piece = w_ref.shape[0] // pieces
+    width = w_ref.shape[1]
+
+    def ctx(zz, yy, cc):
+        return (zz * 2 + yy) * 2 + cc
+
+    def remote(src, dst, ssem, rsem, zz, yy, cc, hh):
+        return pltpu.make_async_remote_copy(
+            src_ref=src, dst_ref=dst, send_sem=ssem, recv_sem=rsem,
+            device_id=(ctx(zz, yy, cc), hh), device_id_type=MESH,
+        )
+
+    def order(i):
+        return i + 1 - 2 * (i % 2)
+
+    own_w = pltpu.make_async_copy(w_ref, wv.at[h, c], loc.at[0])
+    own_w.start()
+
+    def lanes(index):
+        return pl.ds(pl.multiple_of(index * head_size, head_size), head_size)
+
+    def slot(kind, zz, yy, cc):
+        where = ctx(zz, yy, cc)
+        if kind == 0:
+            return kc.at[:, pl.ds(pl.multiple_of(where * cached_rows, cached_rows), cached_rows), :]
+        return kf.at[:, pl.ds(pl.multiple_of(where * rows, rows), rows), :]
+
+    own_c = pltpu.make_async_copy(cached_ref.at[:, :, lanes(z)], slot(0, z, y, c), loc.at[1])
+    own_c.start()
+
+    cosine = cos_ref[...]
+    sine = sin_ref[...]
+
+    def rotate(x):
+        x = x.astype(jnp.float32)
+        return (x * cosine + pltpu.roll(x, head_size // 2, 1) * sine).astype(jnp.bfloat16)
+
+    for g in range(depth):
+        part = slice(g * head_size, (g + 1) * head_size)
+        frot[g, 0] = rotate(fresh_ref[0, :, part])
+        frot[g, 1] = fresh_ref[1, :, part]
+    for j in range(depth * group):
+        part = slice(j * head_size, (j + 1) * head_size)
+        qrot[j // group, j % group] = rotate(q_ref[:, part])
+    qall[z] = qrot[z]
+    own_f = pltpu.make_async_copy(frot.at[z], slot(1, z, y, c), loc.at[2])
+    own_f.start()
+
+    barrier = pltpu.get_barrier_semaphore()
+    for d in range(chips):
+        for e in range(heads):
+            if d or e:
+                pl.semaphore_signal(
+                    barrier, inc=1,
+                    device_id=(lax.rem(chip + d, chips) * 2 + c, lax.rem(h + e, heads)),
+                    device_id_type=MESH,
+                )
+    pl.semaphore_signal(barrier, inc=1, device_id=(ctx(z, y, 1 - c), h), device_id_type=MESH)
+    pl.semaphore_wait(barrier, chips * heads)
+
+    def kv_send(d, kind):
+        to = lax.rem(z + d, depth)
+        src = cached_ref.at[:, :, lanes(to)] if kind == 0 else frot.at[to]
+        return remote(
+            src, slot(kind, z, y, c), kvs.at[d, kind], kvr.at[kind, ctx(z, y, c)], to, y, c, h
+        )
+
+    def kv_pair(zz, kind):
+        where = slot(kind, zz, y, c)
+        return remote(where, where, kys.at[zz, kind], kvr.at[kind, ctx(zz, y, c)], z, 1 - y, c, h)
+
+    def kv_core(zz, yy, kind):
+        where = slot(kind, zz, yy, c)
+        return remote(
+            where, where, kcs.at[zz * 2 + yy, kind], kvr.at[kind, ctx(zz, yy, c)], z, y, 1 - c, h
+        )
+
+    def kv_landed(zz, yy, cc, kind):
+        where = slot(kind, zz, yy, cc)
+        remote(
+            where, where, kcs.at[0, 0], kvr.at[kind, ctx(zz, yy, cc)], z, 1 - y, c, h
+        ).wait_recv()
+
+    def q_send(d):
+        to = lax.rem(z + d, depth)
+        return remote(qrot.at[to], qall.at[z], qs.at[d], qr.at[z], to, y, c, h)
+
+    def w_send(k):
+        part = pl.ds(pl.multiple_of(k * piece, piece), piece)
+        return remote(
+            w_ref.at[part, :], wv.at[h, c, part, :], ws.at[k], wr.at[k], z, y, c, 1 - h
+        )
+
+    def w_forward(k):
+        part = pl.ds(pl.multiple_of(k * piece, piece), piece)
+        where = wv.at[1 - h, c, part, :]
+        return remote(where, where, wfs.at[k], wfr.at[k], z, y, 1 - c, h)
+
+    def w_landed(k):
+        part = pl.ds(pl.multiple_of(k * piece, piece), piece)
+        where = wv.at[1 - h, c, part, :]
+        remote(where, where, wfs.at[k], wr.at[k], z, y, c, 1 - h).wait_recv()
+
+    def w_forwarded(k):
+        part = pl.ds(pl.multiple_of(k * piece, piece), piece)
+        where = wv.at[1 - h, 1 - c, part, :]
+        remote(where, where, wfs.at[k], wfr.at[k], z, y, 1 - c, h).wait_recv()
+
+    own_w_core = remote(w_ref, wv.at[h, c], wos.at[0], wor.at[0], z, y, 1 - c, h)
+
+    first = order(0)
+    for d in range(1, depth):
+        for kind in range(2):
+            kv_send(d, kind).start()
+    for k in range(early):
+        w_send(k).start()
+
+    @pl.when(z == first)
+    def _():
+        for d in range(1, depth):
+            q_send(d).start()
+
+    own_c.wait()
+    own_f.wait()
+    for kind in range(2):
+        kv_pair(z, kind).start()
+        kv_core(z, y, kind).start()
+    for s in range(1, depth):
+        for sign in (-1, 1):
+            zz = z + sign * s
+
+            @pl.when((zz >= 0) & (zz < depth))
+            def _():
+                for kind in range(2):
+                    kv_landed(zz, y, c, kind)
+                    kv_pair(zz, kind).start()
+                    kv_core(zz, y, kind).start()
+
+    @pl.when(z != first)
+    def _():
+        for d in range(1, depth):
+            q_send(d).start()
+
+    for zz in range(depth):
+        for kind in range(2):
+            kv_landed(zz, 1 - y, c, kind)
+            kv_core(zz, 1 - y, kind).start()
+    for zz in range(depth):
+        for yy in range(2):
+            for kind in range(2):
+                kv_landed(zz, yy, 1 - c, kind)
+    own_w_core.start()
+
+    def x_send(e):
+        zp = order(e)
+        return remote(st.at[e], av.at[zp, h, z, y], xs.at[e], xr.at[e], z, y, c, 1 - h)
+
+    def x_landed(e):
+        zp = order(e)
+        remote(st.at[e], av.at[zp, 1 - h, z, y], xs.at[e], xr.at[e], z, y, c, 1 - h).wait_recv()
+
+    def up(e, zz):
+        where = av.at[order(e), :, zz, y]
+        return remote(where, where, us.at[e, zz], zr.at[e, zz], z + 1, y, c, h)
+
+    def down(e, zz):
+        where = av.at[order(e), :, zz, y]
+        return remote(where, where, ds.at[e, zz], zr.at[e, zz], z - 1, y, c, h)
+
+    def across(e, zz):
+        where = av.at[order(e), :, zz, y]
+        return remote(where, where, ys.at[e, zz], yr.at[e, zz], z, 1 - y, c, h)
+
+    def own_out(e):
+        x_landed(e)
+
+        @pl.when(z + 1 < depth)
+        def _():
+            up(e, z).start()
+
+        @pl.when(z >= 1)
+        def _():
+            down(e, z).start()
+
+        across(e, z).start()
+
+    def chain_landed(e, zz):
+        where = av.at[order(e), :, zz, y]
+        remote(where, where, ys.at[e, zz], zr.at[e, zz], z, 1 - y, c, h).wait_recv()
+
+    def hop(e, s):
+        @pl.when(z >= s)
+        def _():
+            chain_landed(e, z - s)
+
+            @pl.when(z + 1 < depth)
+            def _():
+                up(e, z - s).start()
+
+            across(e, z - s).start()
+
+        @pl.when(z + s < depth)
+        def _():
+            chain_landed(e, z + s)
+
+            @pl.when(z >= 1)
+            def _():
+                down(e, z + s).start()
+
+            across(e, z + s).start()
+
+    def across_landed(e):
+        for zz in range(depth):
+            where = av.at[order(e), :, zz, 1 - y]
+            remote(where, where, ys.at[e, zz], yr.at[e, zz], z, 1 - y, c, h).wait_recv()
+
+    scale = LOG2E * head_size ** (-0.5)
+    both = 2 * rows
+    lane_groups = key_block // head_size
+    cached_blocks = kc.shape[1] // key_block
+
+    def attend_pair(i, p):
+        zp = order(i)
+        q = qall[zp, pl.ds(2 * p, 2)].reshape(both, head_size)
+        block = ctx(zp, y, c)
+        fresh_blocks = (block * rows + rows + key_block - 1) // key_block
+
+        def scores(keys):
+            return lax.dot_general(
+                q, keys, (((1,), (1,)), ((), ())), preferred_element_type=jnp.float32
+            )
+
+        def widen(s, top):
+            for u in range(lane_groups):
+                top = jnp.maximum(top, s[:, u * head_size : (u + 1) * head_size])
+            return top
+
+        top = jnp.full((both, head_size), -1e30, jnp.float32)
+        for b in range(cached_blocks):
+            s = scores(kc[0, b * key_block : (b + 1) * key_block, :])
+            s_ref[b] = s
+            top = widen(s, top)
+
+        def fresh_scores(b, top):
+            keys = kf[0, pl.ds(pl.multiple_of(b * key_block, key_block), key_block), :]
+            s = scores(keys)
+            key_pos = b * key_block + lax.broadcasted_iota(jnp.int32, (rows, key_block), 1)
+            query_pos = block * rows + lax.broadcasted_iota(jnp.int32, (rows, key_block), 0)
+            visible = key_pos <= query_pos
+            s = jnp.where(jnp.concatenate([visible, visible], axis=0), s, -1e30)
+            s_ref[cached_blocks + b] = s
+            return widen(s, top)
+
+        top = lax.fori_loop(0, fresh_blocks, fresh_scores, top)
+        peak = jnp.max(top, axis=1, keepdims=True)
+
+        def weigh(s, values, total, summed):
+            e = jnp.exp2((s - peak) * scale)
+            for u in range(lane_groups):
+                total = total + e[:, u * head_size : (u + 1) * head_size]
+            summed = summed + jnp.dot(
+                e.astype(jnp.bfloat16), values, preferred_element_type=jnp.float32
+            )
+            return total, summed
+
+        total = jnp.zeros((both, head_size), jnp.float32)
+        summed = jnp.zeros((both, head_size), jnp.float32)
+        for b in range(cached_blocks):
+            total, summed = weigh(
+                s_ref[b], kc[1, b * key_block : (b + 1) * key_block, :], total, summed
+            )
+
+        def fresh_weigh(b, carry):
+            values = kf[1, pl.ds(pl.multiple_of(b * key_block, key_block), key_block), :]
+            return weigh(s_ref[cached_blocks + b], values, *carry)
+
+        total, summed = lax.fori_loop(0, fresh_blocks, fresh_weigh, (total, summed))
+        out = (summed / jnp.sum(total, axis=1, keepdims=True)).astype(jnp.bfloat16)
+        for a in range(2):
+            upper = out[a * rows : a * rows + half]
+            lower = out[a * rows + half : (a + 1) * rows]
+            where = pl.ds(pl.multiple_of((2 * p + a) * head_size, head_size), head_size)
+            av[zp, h, z, y, :, where] = jnp.where(h == 0, upper, lower)
+            st[i, :, where] = jnp.where(h == 0, lower, upper)
+
+    def step(t, carry):
+        i = t // pair_blocks
+        p = t % pair_blocks
+
+        @pl.when((p == 0) & (order(i) != z))
+        def _():
+            zp = order(i)
+            remote(qrot.at[0], qall.at[zp], qs.at[0], qr.at[zp], z, 1 - y, c, h).wait_recv()
+
+        attend_pair(i, p)
+
+        @pl.when((p == 0) & (i >= 1))
+        def _():
+            x_send(i - 1).start()
+
+        @pl.when(p >= 1)
+        def _():
+            w_send(early + 3 * i + p - 1).start()
+
+        @pl.when((p == 1) & (i >= 1))
+        def _():
+            own_out(i - 1)
+            low = jnp.where(i == 1, 0, early + 3 * (i - 2))
+
+            def forward(k, carry):
+                w_landed(k)
+                w_forward(k).start()
+                return carry
+
+            lax.fori_loop(low, early + 3 * (i - 1), forward, 0)
+
+        @pl.when((p == 3) & (i >= 1))
+        def _():
+            hop(i - 1, 1)
+
+        if depth > 2:
+            @pl.when((p == 1) & (i >= 2))
+            def _():
+                hop(i - 2, 2)
+
+            @pl.when((p == 3) & (i >= 2))
+            def _():
+                for s in range(3, depth):
+                    hop(i - 2, s)
+
+        return carry
+
+    lax.fori_loop(0, depth * pair_blocks, step, 0)
+
+    owner = chip // per
+    place = chip % per
+
+    def tile_send(e, yy):
+        zp = order(e)
+        return remote(
+            cst.at[e, yy], crecv.at[h, place], cs.at[e, yy], cr.at[h, place], zp, yy, c, owner
+        )
+
+    def is_self(e, yy):
+        return (order(e) == z) & (y == yy) & (owner == h)
+
+    def project(e):
+        zp = order(e)
+        across_landed(e)
+        acc_ref[...] = jnp.zeros_like(acc_ref)
+        span = av.shape[5]
+
+        def term(k, carry):
+            xx = k // depth
+            zz = k % depth
+            left = av[zp, xx, zz].reshape(2 * half, span)
+            for cc in range(2):
+                part = pl.ds(cc * width, width)
+                acc_ref[:, part] += jnp.dot(
+                    left,
+                    wv[xx, cc, pl.ds(pl.multiple_of(zz * span, span), span), :],
+                    preferred_element_type=jnp.float32,
+                )
+            return carry
+
+        lax.fori_loop(0, heads * depth, term, 0)
+        for yy in range(2):
+            cst[e, yy] = acc_ref[yy * half : (yy + 1) * half, :].astype(jnp.bfloat16)
+
+        for yy in range(2):
+            @pl.when(is_self(e, yy))
+            def _():
+                crecv[h, place] = cst[e, yy]
+
+            @pl.when(jnp.logical_not(is_self(e, yy)))
+            def _():
+                tile_send(e, yy).start()
+
+    last = depth - 1
+    x_send(last).start()
+    if depth > 2:
+        hop(last - 1, 2)
+    own_out(last)
+    for s in range(3, depth):
+        hop(last - 1, s)
+
+    def forward(k, carry):
+        w_landed(k)
+        w_forward(k).start()
+        return carry
+
+    hop(last, 1)
+    lax.fori_loop(early + 3 * (depth - 2), pieces, forward, 0)
+    own_w.wait()
+    remote(w_ref, wv.at[h, 1 - c], wos.at[0], wor.at[0], z, y, 1 - c, h).wait_recv()
+
+    def forwarded(k, carry):
+        w_forwarded(k)
+        return carry
+
+    lax.fori_loop(0, pieces, forwarded, 0)
+    for e in range(depth):
+        if e + 2 < depth:
+            project(e)
+            hop(last, e + 2)
+        else:
+            project(e)
+
+    for xx in range(heads):
+        for s in range(per):
+            @pl.when(jnp.logical_not((h * per + s == chip) & (h == xx)))
+            def _():
+                remote(
+                    cst.at[0, 0], crecv.at[xx, s], cs.at[0, 0], cr.at[xx, s], z, 1 - y, c, h
+                ).wait_recv()
+
+            rows_of = slice(xx * half, (xx + 1) * half)
+            columns = slice(s * 2 * width, (s + 1) * 2 * width)
+            out_ref[rows_of, columns] = (
+                hidden_ref[rows_of, columns].astype(jnp.float32)
+                + crecv[xx, s].astype(jnp.float32)
+            ).astype(jnp.bfloat16)
+
+    for d in range(1, depth):
+        for kind in range(2):
+            kv_send(d, kind).wait_send()
+        q_send(d).wait_send()
+    for zz in range(depth):
+        for kind in range(2):
+            kv_pair(zz, kind).wait_send()
+            for yy in range(2):
+                kv_core(zz, yy, kind).wait_send()
+    own_w_core.wait_send()
+
+    def w_sent(k, carry):
+        w_send(k).wait_send()
+        w_forward(k).wait_send()
+        return carry
+
+    lax.fori_loop(0, pieces, w_sent, 0)
+    for e in range(depth):
+        x_send(e).wait_send()
+        for zz in range(depth):
+            across(e, zz).wait_send()
+
+            @pl.when((zz <= z) & (z + 1 < depth))
+            def _():
+                up(e, zz).wait_send()
+
+            @pl.when((zz >= z) & (z >= 1))
+            def _():
+                down(e, zz).wait_send()
+
+        for yy in range(2):
+            @pl.when(jnp.logical_not(is_self(e, yy)))
+            def _():
+                tile_send(e, yy).wait_send()
+
+
+def fused(cosine, sine, query, fresh, cached, weight, hidden, depth, heads):
+    rows, wide = query.shape
+    head_size = HEAD_DIMENSION
+    group = wide // head_size // depth
+    contexts = depth * 4
+    half = rows // heads
+    key_block = 512
+    cached_total = contexts * cached.shape[1]
+    fresh_total = contexts * rows
+    while cached_total % key_block or fresh_total % key_block:
+        key_block //= 2
+    pieces = 4 * depth
+    per = depth * 2 // heads
+    dma = pltpu.SemaphoreType.DMA
+    bf16 = jnp.bfloat16
+    vmem = pltpu.VMEM
+    whole = pl.BlockSpec(memory_space=pltpu.VMEM)
+    far = pl.BlockSpec(memory_space=pl.ANY)
+    return pl.pallas_call(
+        functools.partial(fused_kernel, depth, group, heads, key_block),
+        out_shape=jax.ShapeDtypeStruct(hidden.shape, bf16),
+        in_specs=[whole, whole, whole, whole, far, far, whole],
+        out_specs=whole,
+        scratch_shapes=[
+            vmem((depth, group, rows, head_size), bf16),
+            vmem((depth, group, rows, head_size), bf16),
+            vmem((depth, 2, rows, head_size), bf16),
+            vmem((2, cached_total, head_size), bf16),
+            vmem((2, fresh_total, head_size), bf16),
+            vmem(((cached_total + fresh_total) // key_block, 2 * rows, key_block), jnp.float32),
+            vmem((depth, heads, depth, 2, half, group * head_size), bf16),
+            vmem((depth, half, group * head_size), bf16),
+            vmem((heads, 2) + weight.shape, bf16),
+            vmem((rows, 2 * weight.shape[1]), jnp.float32),
+            vmem((depth, 2, half, 2 * weight.shape[1]), bf16),
+            vmem((heads, per, half, 2 * weight.shape[1]), bf16),
+            dma((depth, 2)), dma((2, contexts)), dma((depth, 2)), dma((depth * 2, 2)),
+            dma((3,)), dma((depth,)), dma((depth,)),
+            dma((pieces,)), dma((pieces,)), dma((1,)), dma((1,)), dma((pieces,)), dma((pieces,)),
+            dma((depth,)), dma((depth,)),
+            dma((depth, depth)), dma((depth, depth)), dma((depth, depth)),
+            dma((depth, depth)), dma((depth, depth)),
+            dma((depth, 2)), dma((heads, per)),
+        ],
+        compiler_params=pltpu.CompilerParams(
+            collective_id=2, has_side_effects=True, vmem_limit_bytes=60 * 1024 * 1024
+        ),
+    )(cosine, sine, query, fresh, cached, weight, hidden)
+
+
 def exchange(x, axis_name, size):
     return lax.ppermute(x, axis_name, [(i, i ^ 1) for i in range(size)])
 
@@ -371,17 +903,6 @@
     core = me % cores
     head = lax.axis_index("head")
     cosine_table, sine_table = tables(positions, head_size)
-    rotary_query_rows = apply_rotary(
-        query.astype(jnp.float32).reshape(new_rows, q_local, head_size), cosine_table, sine_table
-    ).astype(jnp.bfloat16).reshape(new_rows, q_local * head_size)
-    rotary_key_rows = apply_rotary(
-        fresh_key_value[0].astype(jnp.float32).reshape(new_rows, kv_local, head_size),
-        cosine_table,
-        sine_table,
-    ).astype(jnp.bfloat16)
-    recent = jnp.stack(
-        [rotary_key_rows.reshape(new_rows, kv_local * head_size), fresh_key_value[1]]
-    )
     if heads == 2:
         other_gain = exchange(norm_gain, "head", heads)
         whole_gain = jnp.concatenate(
@@ -389,22 +910,46 @@
         )
     else:
         whole_gain = lax.all_gather(norm_gain, "head", axis=0, tiled=True)
-    other_weight = exchange(out_weight, "ctx", contexts)
-    first_row = me * new_rows
-    cached_all = lax.all_gather(cached_key_value, "ctx", axis=1, tiled=True)
-    recent_all = lax.all_gather(recent, "ctx", axis=1, tiled=True)
-    state = attend(rotary_query_rows, cached_all, first_row, None, head_size)
-    attn = attend(rotary_query_rows, recent_all, first_row, tuple(state), head_size)
-    outputs = gather_rows(attn, chips, cores)
-    own = jnp.dot(outputs, out_weight, preferred_element_type=jnp.float32).astype(jnp.bfloat16)
-    other = jnp.dot(outputs, other_weight, preferred_element_type=jnp.float32).astype(jnp.bfloat16)
-    product = jnp.concatenate(
-        [jnp.where(core == 0, own, other), jnp.where(core == 0, other, own)], axis=1
-    ).reshape(chips, new_rows, -1)
-    parts = scatter_columns(product, chips, cores, heads)
-    head_summed = jnp.sum(parts.astype(jnp.float32), axis=0)
-    head_summed = head_summed.transpose(1, 0, 2).reshape(hidden.shape)
-    layer2_out = (hidden.astype(jnp.float32) + head_summed).astype(jnp.bfloat16)
+    if heads == 2 and kv_local * 2 == chips and q_local == 8 * kv_local:
+        layer2_out = fused(
+            jnp.concatenate([cosine_table, cosine_table], axis=1),
+            jnp.concatenate([-sine_table, sine_table], axis=1),
+            query,
+            fresh_key_value,
+            cached_key_value,
+            out_weight,
+            hidden,
+            kv_local,
+            heads,
+        )
+    else:
+        rotary_query_rows = apply_rotary(
+            query.astype(jnp.float32).reshape(new_rows, q_local, head_size), cosine_table, sine_table
+        ).astype(jnp.bfloat16).reshape(new_rows, q_local * head_size)
+        rotary_key_rows = apply_rotary(
+            fresh_key_value[0].astype(jnp.float32).reshape(new_rows, kv_local, head_size),
+            cosine_table,
+            sine_table,
+        ).astype(jnp.bfloat16)
+        recent = jnp.stack(
+            [rotary_key_rows.reshape(new_rows, kv_local * head_size), fresh_key_value[1]]
+        )
+        other_weight = exchange(out_weight, "ctx", contexts)
+        first_row = me * new_rows
+        cached_all = lax.all_gather(cached_key_value, "ctx", axis=1, tiled=True)
+        recent_all = lax.all_gather(recent, "ctx", axis=1, tiled=True)
+        state = attend(rotary_query_rows, cached_all, first_row, None, head_size)
+        attn = attend(rotary_query_rows, recent_all, first_row, tuple(state), head_size)
+        outputs = gather_rows(attn, chips, cores)
+        own = jnp.dot(outputs, out_weight, preferred_element_type=jnp.float32).astype(jnp.bfloat16)
+        other = jnp.dot(outputs, other_weight, preferred_element_type=jnp.float32).astype(jnp.bfloat16)
+        product = jnp.concatenate(
+            [jnp.where(core == 0, own, other), jnp.where(core == 0, other, own)], axis=1
+        ).reshape(chips, new_rows, -1)
+        parts = scatter_columns(product, chips, cores, heads)
+        head_summed = jnp.sum(parts.astype(jnp.float32), axis=0)
+        head_summed = head_summed.transpose(1, 0, 2).reshape(hidden.shape)
+        layer2_out = (hidden.astype(jnp.float32) + head_summed).astype(jnp.bfloat16)
     if heads == 2:
         other_out = exchange(layer2_out, "head", heads)
         whole_out = jnp.concatenate(

time: 463 us -> 235 us (0.51)
  the two profiles are of different devices: /device:TPU:28 before, /device:TPU:22 now
where the time goes in v1:
time: 235 us; the launch traced here: 234 us
  Pallas kernels  195 us (83%)
  waiting for transfers between devices  18.4 us (8%)
  matrix products  8.27 us (4%)
  other arithmetic  5.41 us (2%)
  local copies, waits for them, and re-layouts  3.24 us (1%)
    pallas_call x1, Pallas kernels, fused(): pl.pallas_call(functools.partial(fused_kernel, depth, group, heads, key_b...  195 us
    ppermute x2, waiting for transfers between devices, exchange(): return lax.ppermute(x, axis_name, [(i, i ^ 1) for i in range(size)])  18.4 us
    dot_general x1, matrix products, local(): jnp.dot(full_rows, layer3_key_value_weight, preferred_element_type=jnp.fl...  8.27 us
  transfers between devices with their start and end apart: 2, of which 1 were waited for; matrix products, arithmetic and copies ran while one was open for 0% of the time, Pallas kernels for 0%

profile of v1, /device:TPU:22, one launch (start us, length us, event | category | flops | bytes accessed | tf_op | source)
XLA Modules:
  0.0 234.4 jit_solution(9212787701993469741)
XLA Ops:
  0.7 0.7 convert_element_type.46
  1.4 0.3 fusion.5
  1.7 0.8 pad_maximum_fusion.2
  2.5 0.0 copy-start.1
  2.5 0.0 copy-start.3
  2.5 195.5 %shard_map.122 = bf16[128,4096]{1,0:T(8,128)(2,1)} custom-call(f32[128,128]{1,0:T(8,128)} %get-tuple-element.14.refs_0_, f32[128,128]{1,0:T(8,128)} %get-tuple-element.15.refs_1_, bf16[128,4096]{1,0:T(8,128)(2,1)} %refs_2_.1, bf16[2,128,512]{2,1,0:T(8,128)(2,1)} %refs_3_.1, bf16[2,256,512]{2,1,0:T(8,128)(2,1)} %refs_4_.1, bf16[4096,512]{1,0:T(8,128)(2,1)} %refs_5_.1, ...), custom_call_target="tpu_custom_call" | custom-call | tf_op jit(solution)/shard_map/pallas_call | solution.py:845
  197.9 0.1 collective-permute-start
  198.0 0.0 copy-done.1
  198.0 2.0 collective-permute-start.1
  200.7 0.0 copy-done.3
  200.7 18.4 %collective-permute-done.1 = f32[4096]{0:T(1024)S(1)} collective-permute-done((f32[4096]{0:T(1024)S(1)}, f32[4096]{0:T(1024)S(1)}, u32[]{:S(2)}, u32[]{:S(2)}) %collective-permute-start.1) | collective-permute-done | bytes 16416 | tf_op jit(solution)/shard_map/ppermute | solution.py:878
  219.2 0.0 collective-permute-done
  219.2 1.4 broadcast_select_fusion.1
  220.6 0.0 copy-start.2
  220.6 0.5 fusion
  221.1 0.6 fusion.2
  221.7 0.0 copy-done.2
  221.7 8.3 %convolution_add_fusion = f32[128,1024]{1,0:T(8,128)S(1)} fusion(bf16[128,8192]{1,0:T(8,128)(2,1)S(1)} %fusion.2, bf16[8192,1024]{1,0:T(8,128)(2,1)} %param.18, f32[1024]{0:T(1024)S(1)} %copy-done.2), kind=kOutput, calls=%fused_computation.7 | convolution fusion | flops 2147614720 | bytes 19402752 | tf_op jit(solution)/shard_map/dot_general | solution.py:970
  230.0 0.0 copy-start
  230.0 0.4 reshape.200
  230.4 0.2 slice.31
  230.6 0.3 slice.34
  230.9 0.1 subtract_convert_fusion
  231.1 0.1 maximum_bitcast_fusion
  231.3 0.3 copy.16
  231.5 0.2 convert_element_type.50
  231.7 0.9 gather_fusion
  232.6 0.8 select_select_fusion
  233.4 0.0 copy-done
  233.4 1.0 copy.25
  (13 shorter events, 0.1 us)
Async XLA Ops:
  2.5 195.5 %copy-start.1 = (f32[4096]{0:T(1024)S(1)}, f32[4096]{0:T(1024)}, u32[]{:S(2)}) copy-start(f32[4096]{0:T(1024)} %param.17) | copy-start | bytes 49156
  2.5 198.2 %copy-start.3 = (s32[128]{0:T(128)S(1)}, s32[128]{0:T(128)}, u32[]{:S(2)}) copy-start(s32[128]{0:T(128)} %param.20) | copy-start | bytes 1540
  197.9 21.2 %collective-permute-start = (bf16[128,4096]{1,0:T(8,128)(2,1)}, bf16[128,4096]{1,0:T(8,128)(2,1)S(1)}, u32[]{:S(2)}, u32[]{:S(2)}) collective-permute-start(bf16[128,4096]{1,0:T(8,128)(2,1)} %shard_map.122), channel_id=1, source_target_pairs={{0,1},{1,0},{2,3},{3,2},{4,5},{5,4},{6,7},{7,6},{8,9},{9,8},{10,11... | collective-permute-start | bytes 3145736 | tf_op jit(solution)/shard_map/ppermute | solution.py:878
  198.0 21.1 %collective-permute-start.1 = (f32[4096]{0:T(1024)S(1)}, f32[4096]{0:T(1024)S(1)}, u32[]{:S(2)}, u32[]{:S(2)}) collective-permute-start(f32[4096]{0:T(1024)S(1)} %copy-done.1), channel_id=1, source_target_pairs={{0,1},{1,0},{2,3},{3,2},{4,5},{5,4},{6,7},{7,6},{8,9},{9,8},{10,11... | collective-permute-start | bytes 49160 | tf_op jit(solution)/shard_map/ppermute | solution.py:878
  220.6 1.1 copy-start.2
  230.0 3.4 %copy-start = (bf16[128,4096]{1,0:T(8,128)(2,1)S(1)}, bf16[128,4096]{1,0:T(8,128)(2,1)}, u32[]{:S(2)}) copy-start(bf16[128,4096]{1,0:T(8,128)(2,1)} %shard_map.122) | copy-start | bytes 3145732

commit v2 on v0

--- a/solution.py
+++ b/solution.py
@@ -342,6 +342,589 @@
     )(halves).reshape(chips * rows, width)
 
 
+MESH = pl.DeviceIdType.MESH
+EARLY = 4
+QUARTERS = 4
+
+
+def fused_kernel(depth, group, heads, key_block, *refs):
+    (cos_ref, sin_ref, q_ref, fresh_ref, hidden_ref, gain_ref, bias_ref, keep_ref, count_ref,
+     cached_ref, w_ref, w3_ref, out_ref, packed_ref,
+     qrot, qall, frot, kc, kf, s_ref, av, st, wv, w3, acc_ref, cst, crecv, rows_ref, gains,
+     kvs, kvr, kys, kcs, loc, qs, qr, ws, wr, wos, wor, wfs, wfr,
+     xs, xr, us, ds, ys, zr, yr, cs, cr, ls, lr, gs, gr) = refs
+    rows = q_ref.shape[0]
+    head_size = kc.shape[2]
+    quarter = rows // QUARTERS
+    half = quarter // heads
+    cached_rows = cached_ref.shape[1]
+    chips = depth * 2
+    per = chips // heads
+    me = lax.axis_index("ctx")
+    h = lax.axis_index("head")
+    chip = me // 2
+    c = me % 2
+    z = chip // 2
+    y = chip % 2
+    pieces = ws.shape[0]
+    piece = w_ref.shape[0] // pieces
+    width = w_ref.shape[1]
+    last = QUARTERS - 1
+
+    def ctx(zz, yy, cc):
+        return (zz * 2 + yy) * 2 + cc
+
+    def remote(src, dst, ssem, rsem, zz, yy, cc, hh):
+        return pltpu.make_async_remote_copy(
+            src_ref=src, dst_ref=dst, send_sem=ssem, recv_sem=rsem,
+            device_id=(ctx(zz, yy, cc), hh), device_id_type=MESH,
+        )
+
+    def landed(where, rsem):
+        remote(where, where, ls.at[0], rsem, z, 1 - y, c, h).wait_recv()
+
+    barrier = pltpu.get_barrier_semaphore()
+    for d in range(chips):
+        for e in range(heads):
+            if d or e:
+                pl.semaphore_signal(
+                    barrier, inc=1,
+                    device_id=(lax.rem(chip + d, chips) * 2 + c, lax.rem(h + e, heads)),
+                    device_id_type=MESH,
+                )
+    pl.semaphore_signal(barrier, inc=1, device_id=(ctx(z, y, 1 - c), h), device_id_type=MESH)
+
+    def lanes(index):
+        return pl.ds(pl.multiple_of(index * head_size, head_size), head_size)
+
+    def slot(kind, zz, yy, cc):
+        where = ctx(zz, yy, cc)
+        if kind == 0:
+            return kc.at[:, pl.ds(pl.multiple_of(where * cached_rows, cached_rows), cached_rows), :]
+        return kf.at[:, pl.ds(pl.multiple_of(where * rows, rows), rows), :]
+
+    own_c = pltpu.make_async_copy(cached_ref.at[:, :, lanes(z)], slot(0, z, y, c), loc.at[0])
+    own_c.start()
+    own_w = pltpu.make_async_copy(w_ref, wv.at[h, c], loc.at[1])
+    own_w.start()
+
+    cosine = cos_ref[...]
+    sine = sin_ref[...]
+
+    def rotate(x):
+        x = x.astype(jnp.float32)
+        return x * cosine + pltpu.roll(x, head_size // 2, 1) * sine
+
+    for g in range(depth):
+        part = slice(g * head_size, (g + 1) * head_size)
+        frot[g, 0] = rotate(fresh_ref[0, :, part]).astype(jnp.bfloat16)
+        frot[g, 1] = fresh_ref[1, :, part]
+    own_f = pltpu.make_async_copy(frot.at[z], slot(1, z, y, c), loc.at[2])
+    own_f.start()
+
+    def kv_send(d, kind):
+        to = lax.rem(z + d, depth)
+        src = cached_ref.at[:, :, lanes(to)] if kind == 0 else frot.at[to]
+        return remote(
+            src, slot(kind, z, y, c), kvs.at[d, kind], kvr.at[kind, ctx(z, y, c)], to, y, c, h
+        )
+
+    def kv_pair(zz, kind):
+        where = slot(kind, zz, y, c)
+        return remote(where, where, kys.at[zz, kind], kvr.at[kind, ctx(zz, y, c)], z, 1 - y, c, h)
+
+    def kv_core(zz, yy, kind):
+        where = slot(kind, zz, yy, c)
+        return remote(
+            where, where, kcs.at[zz * 2 + yy, kind], kvr.at[kind, ctx(zz, yy, c)], z, y, 1 - c, h
+        )
+
+    def kv_landed(zz, yy, cc, kind):
+        landed(slot(kind, zz, yy, cc), kvr.at[kind, ctx(zz, yy, cc)])
+
+    def q_send(i, d):
+        to = lax.rem(z + d, depth)
+        return remote(qrot.at[to, i], qall.at[i, z], qs.at[i, d], qr.at[i, z], to, y, c, h)
+
+    def w_part(k):
+        return pl.ds(pl.multiple_of(k * piece, piece), piece)
+
+    def w_send(k):
+        return remote(
+            w_ref.at[w_part(k), :], wv.at[h, c, w_part(k), :], ws.at[k], wr.at[k], z, y, c, 1 - h
+        )
+
+    def w_forward(k):
+        where = wv.at[1 - h, c, w_part(k), :]
+        return remote(where, where, wfs.at[k], wfr.at[k], z, y, 1 - c, h)
+
+    def forward(k, carry):
+        landed(wv.at[1 - h, c, w_part(k), :], wr.at[k])
+        w_forward(k).start()
+        return carry
+
+    own_w_core = remote(w_ref, wv.at[h, c], wos.at[0], wor.at[0], z, y, 1 - c, h)
+    gain_send = remote(gain_ref, gains.at[h], gs.at[0], gr.at[0], z, y, c, 1 - h)
+
+    pl.semaphore_wait(barrier, chips * heads)
+    for kind in range(2):
+        for d in range(1, depth):
+            kv_send(d, kind).start()
+    for k in range(EARLY):
+        w_send(k).start()
+    own_c.wait()
+    own_f.wait()
+    for kind in range(2):
+        kv_pair(z, kind).start()
+        kv_core(z, y, kind).start()
+
+    for j in range(depth * group):
+        x = rotate(q_ref[:, j * head_size : (j + 1) * head_size]).astype(jnp.bfloat16)
+        for i in range(QUARTERS):
+            qrot[j // group, i, j % group] = x[i * quarter : (i + 1) * quarter]
+    for i in range(QUARTERS):
+        qall[i, z] = qrot[z, i]
+
+    for s in range(1, depth):
+        for sign in (-1, 1):
+            zz = z + sign * s
+
+            @pl.when((zz >= 0) & (zz < depth))
+            def _():
+                for kind in range(2):
+                    kv_landed(zz, y, c, kind)
+                    kv_pair(zz, kind).start()
+                    kv_core(zz, y, kind).start()
+
+        if s == 1:
+            for i in range(QUARTERS):
+                for d in range(1, depth):
+                    q_send(i, d).start()
+
+    for zz in range(depth):
+        for kind in range(2):
+            kv_landed(zz, 1 - y, c, kind)
+            kv_core(zz, 1 - y, kind).start()
+    gain_send.start()
+    for zz in range(depth):
+        for yy in range(2):
+            for kind in range(2):
+                kv_landed(zz, yy, 1 - c, kind)
+    own_w_core.start()
+    own_w3 = pltpu.make_async_copy(w3_ref, w3, loc.at[3])
+    own_w3.start()
+
+    def side(w):
+        return lax.rem(h + w, 2)
+
+    def x_send(e):
+        return remote(st.at[e], av.at[e, h, z, y], xs.at[e], xr.at[e], z, y, c, 1 - h)
+
+    def unit(e, w, zz, yy):
+        return av.at[e, side(w), zz, yy]
+
+    def up(e, w, zz):
+        where = unit(e, w, zz, y)
+        return remote(where, where, us.at[e, w, zz], zr.at[e, w, zz], z + 1, y, c, h)
+
+    def down(e, w, zz):
+        where = unit(e, w, zz, y)
+        return remote(where, where, ds.at[e, w, zz], zr.at[e, w, zz], z - 1, y, c, h)
+
+    def across(e, w, zz):
+        where = unit(e, w, zz, y)
+        return remote(where, where, ys.at[e, w, zz], yr.at[e, w, zz], z, 1 - y, c, h)
+
+    def own_out(e, w):
+        if w:
+            landed(unit(e, w, z, y), xr.at[e])
+
+        @pl.when(z + 1 < depth)
+        def _():
+            up(e, w, z).start()
+
+        @pl.when(z >= 1)
+        def _():
+            down(e, w, z).start()
+
+        across(e, w, z).start()
+
+    def hop(e, w, s):
+        @pl.when(z >= s)
+        def _():
+            landed(unit(e, w, z - s, y), zr.at[e, w, z - s])
+
+            @pl.when(z + 1 < depth)
+            def _():
+                up(e, w, z - s).start()
+
+            across(e, w, z - s).start()
+
+        @pl.when(z + s < depth)
+        def _():
+            landed(unit(e, w, z + s, y), zr.at[e, w, z + s])
+
+            @pl.when(z >= 1)
+            def _():
+                down(e, w, z + s).start()
+
+            across(e, w, z + s).start()
+
+    scale = LOG2E * head_size ** (-0.5)
+    both = group * quarter
+    lane_groups = key_block // head_size
+    cached_blocks = kc.shape[1] // key_block
+
+    def attend(i, zp):
+        q = qall[i, zp].reshape(both, head_size)
+        start = ctx(zp, y, c) * rows + i * quarter
+        fresh_blocks = (start + quarter + key_block - 1) // key_block
+
+        def scores(keys):
+            return lax.dot_general(
+                q, keys, (((1,), (1,)), ((), ())), preferred_element_type=jnp.float32
+            )
+
+        def widen(s, top):
+            for u in range(lane_groups):
+                top = jnp.maximum(top, s[:, u * head_size : (u + 1) * head_size])
+            return top
+
+        top = jnp.full((both, head_size), -1e30, jnp.float32)
+        for b in range(cached_blocks):
+            s = scores(kc[0, b * key_block : (b + 1) * key_block, :])
+            s_ref[b] = s
+            top = widen(s, top)
+
+        def fresh_scores(b, top):
+            keys = kf[0, pl.ds(pl.multiple_of(b * key_block, key_block), key_block), :]
+            s = scores(keys)
+            key_pos = b * key_block + lax.broadcasted_iota(jnp.int32, (quarter, key_block), 1)
+            query_pos = start + lax.broadcasted_iota(jnp.int32, (quarter, key_block), 0)
+            visible = key_pos <= query_pos
+            s = jnp.where(jnp.concatenate([visible] * group, axis=0), s, -1e30)
+            s_ref[cached_blocks + b] = s
+            return widen(s, top)
+
+        top = lax.fori_loop(0, fresh_blocks, fresh_scores, top)
+        peak = jnp.max(top, axis=1, keepdims=True)
+
+        def weigh(s, values, total, summed):
+            e = jnp.exp2((s - peak) * scale)
+            for u in range(lane_groups):
+                total = total + e[:, u * head_size : (u + 1) * head_size]
+            summed = summed + jnp.dot(
+                e.astype(jnp.bfloat16), values, preferred_element_type=jnp.float32
+            )
+            return total, summed
+
+        total = jnp.zeros((both, head_size), jnp.float32)
+        summed = jnp.zeros((both, head_size), jnp.float32)
+        for b in range(cached_blocks):
+            total, summed = weigh(
+                s_ref[b], kc[1, b * key_block : (b + 1) * key_block, :], total, summed
+            )
+
+        def fresh_weigh(b, carry):
+            values = kf[1, pl.ds(pl.multiple_of(b * key_block, key_block), key_block), :]
+            return weigh(s_ref[cached_blocks + b], values, *carry)
+
+        total, summed = lax.fori_loop(0, fresh_blocks, fresh_weigh, (total, summed))
+        out = (summed / jnp.sum(total, axis=1, keepdims=True)).astype(jnp.bfloat16)
+        where = pl.ds(pl.multiple_of(zp * half, half), half)
+        for a in range(group):
+            upper = out[a * quarter : a * quarter + half]
+            lower = out[a * quarter + half : (a + 1) * quarter]
+            part = slice(a * head_size, (a + 1) * head_size)
+            av[i, h, z, y, where, part] = jnp.where(h == 0, upper, lower)
+            st[i, where, part] = jnp.where(h == 0, lower, upper)
+
+    def step(t, carry):
+        i = t // depth
+        p = t % depth
+        zp = lax.rem(z + p, depth)
+
+        @pl.when(p != 0)
+        def _():
+            landed(qall.at[i, zp], qr.at[i, zp])
+
+        attend(i, zp)
+
+        @pl.when(p >= 1)
+        def _():
+            w_send(EARLY + (depth - 1) * i + p - 1).start()
+
+        @pl.when((p == 0) & (i >= 1))
+        def _():
+            x_send(i - 1).start()
+            own_out(i - 1, 0)
+
+        @pl.when((p == 0) & (i >= 2))
+        def _():
+            hop(i - 2, 0, 2)
+
+        @pl.when((p == 1) & (i >= 1))
+        def _():
+            own_out(i - 1, 1)
+            low = jnp.where(i == 1, 0, EARLY + (depth - 1) * (i - 2))
+            lax.fori_loop(low, EARLY + (depth - 1) * (i - 1), forward, 0)
+
+        @pl.when((p == 1) & (i >= 2))
+        def _():
+            hop(i - 2, 1, 2)
+
+        for w in range(2):
+            @pl.when((p == depth - 2 + w) & (i >= 1))
+            def _():
+                hop(i - 1, w, 1)
+
+            @pl.when((p == depth - 2 + w) & (i >= 2))
+            def _():
+                for s in range(3, depth):
+                    hop(i - 2, w, s)
+
+        return carry
+
+    lax.fori_loop(0, QUARTERS * depth, step, 0)
+
+    owner = chip // per
+    place = chip % per
+    span = av.shape[5]
+
+    def tile_send(e, zp, yy):
+        return remote(
+            cst.at[e, yy, zp], crecv.at[e, h, place], cs.at[e, yy, zp], cr.at[e, h, place],
+            zp, yy, c, owner,
+        )
+
+    def is_self(zp, yy):
+        return (z == zp) & (y == yy) & (owner == h)
+
+    def project(e):
+        for w in range(2):
+            for zz in range(depth):
+                landed(unit(e, w, zz, 1 - y), yr.at[e, w, zz])
+        acc_ref[...] = jnp.zeros_like(acc_ref)
+
+        def term(k, carry):
+            xx = k // depth
+            zz = k % depth
+            left = av[e, xx, zz].reshape(2 * depth * half, span)
+            for cc in range(2):
+                acc_ref[:, cc * width : (cc + 1) * width] += jnp.dot(
+                    left,
+                    wv[xx, cc, pl.ds(pl.multiple_of(zz * span, span), span), :],
+                    preferred_element_type=jnp.float32,
+                )
+            return carry
+
+        lax.fori_loop(0, heads * depth, term, 0)
+        for yy in range(2):
+            for zp in range(depth):
+                low = (yy * depth + zp) * half
+                cst[e, yy, zp] = acc_ref[low : low + half, :].astype(jnp.bfloat16)
+        for yy in range(2):
+            for zp in range(depth):
+                @pl.when(is_self(zp, yy))
+                def _():
+                    crecv[e, h, place] = cst[e, yy, zp]
+
+                @pl.when(jnp.logical_not(is_self(zp, yy)))
+                def _():
+                    tile_send(e, zp, yy).start()
+
+    def rows_send(e):
+        return remote(rows_ref.at[h, e], rows_ref.at[h, e], ls.at[e], lr.at[e], z, y, c, 1 - h)
+
+    def finish(e):
+        for xx in range(heads):
+            for s in range(per):
+                @pl.when(jnp.logical_not((h * per + s == chip) & (h == xx)))
+                def _():
+                    landed(crecv.at[e, xx, s], cr.at[e, xx, s])
+
+                rows_of = slice(e * quarter + xx * half, e * quarter + (xx + 1) * half)
+                columns = slice(s * 2 * width, (s + 1) * 2 * width)
+                done = (
+                    hidden_ref[rows_of, columns].astype(jnp.float32)
+                    + crecv[e, xx, s].astype(jnp.float32)
+                ).astype(jnp.bfloat16)
+                out_ref[rows_of, columns] = done
+                rows_ref[h, e, xx * half : (xx + 1) * half, columns] = done
+        rows_send(e).start()
+
+    x_send(last).start()
+    own_out(last, 0)
+    hop(last - 1, 0, 2)
+    own_out(last, 1)
+    hop(last - 1, 1, 2)
+    for w in range(2):
+        hop(last, w, 1)
+        for s in range(3, depth):
+            hop(last - 1, w, s)
+    lax.fori_loop(EARLY + (depth - 1) * (last - 1), pieces, forward, 0)
+    for s in range(2, depth):
+        for w in range(2):
+            hop(last, w, s)
+    own_w.wait()
+    landed(wv.at[h, 1 - c], wor.at[0])
+
+    def forwarded(k, carry):
+        landed(wv.at[1 - h, 1 - c, w_part(k), :], wfr.at[k])
+        return carry
+
+    lax.fori_loop(0, pieces, forwarded, 0)
+    project(0)
+    for e in range(1, QUARTERS):
+        project(e)
+        finish(e - 1)
+    own_w3.wait()
+    gains[h] = gain_ref[...]
+    landed(gains.at[1 - h], gr.at[0])
+    finish(last)
+
+    for e in range(QUARTERS):
+        landed(rows_ref.at[1 - h, e], lr.at[e])
+    model = rows_ref.shape[3]
+    squares = jnp.zeros((rows, head_size), jnp.float32)
+    for xx in range(heads):
+        for k in range(model // head_size):
+            part = slice(k * head_size, (k + 1) * head_size)
+            x = rows_ref[xx, :, :, part].reshape(rows, head_size).astype(jnp.float32)
+            squares = squares + x * x
+    level = lax.rsqrt(jnp.sum(squares, axis=1, keepdims=True) / (heads * model) + 1e-06)
+    acc_ref[...] = jnp.zeros_like(acc_ref)
+    for xx in range(heads):
+        for k in range(model // span):
+            part = slice(k * span, (k + 1) * span)
+            x = rows_ref[xx, :, :, part].reshape(rows, span).astype(jnp.float32)
+            normed = (x * level * gains[xx, :, part]).astype(jnp.bfloat16)
+            low = xx * model + k * span
+            acc_ref[...] += jnp.dot(
+                normed, w3[low : low + span, :], preferred_element_type=jnp.float32
+            )
+    chosen = keep_ref[...] == lax.broadcasted_iota(jnp.int32, (rows, rows), 1)
+    filled = lax.broadcasted_iota(jnp.int32, (rows, rows), 0) < count_ref[...]
+    pick = jnp.where(chosen & filled, 1.0, 0.0).astype(jnp.bfloat16)
+    for g in range(2 * depth):
+        part = slice(g * head_size, (g + 1) * head_size)
+        x = acc_ref[:, part] + bias_ref[:, part]
+        if g % 2 == 0:
+            x = rotate(x)
+        packed_ref[:, part] = jnp.dot(
+            pick, x.astype(jnp.bfloat16), preferred_element_type=jnp.float32
+        ).astype(jnp.bfloat16)
+
+    for d in range(1, depth):
+        for kind in range(2):
+            kv_send(d, kind).wait_send()
+        for i in range(QUARTERS):
+            q_send(i, d).wait_send()
+    for zz in range(depth):
+        for kind in range(2):
+            kv_pair(zz, kind).wait_send()
+            for yy in range(2):
+                kv_core(zz, yy, kind).wait_send()
+    own_w_core.wait_send()
+    gain_send.wait_send()
+
+    def w_sent(k, carry):
+        w_send(k).wait_send()
+        w_forward(k).wait_send()
+        return carry
+
+    lax.fori_loop(0, pieces, w_sent, 0)
+
+    def sent(e, carry):
+        x_send(e).wait_send()
+        rows_send(e).wait_send()
+        for zz in range(depth):
+            for w in range(2):
+                across(e, w, zz).wait_send()
+
+                @pl.when((zz <= z) & (z + 1 < depth))
+                def _():
+                    up(e, w, zz).wait_send()
+
+                @pl.when((zz >= z) & (z >= 1))
+                def _():
+                    down(e, w, zz).wait_send()
+
+            for yy in range(2):
+                @pl.when(jnp.logical_not(is_self(zz, yy)))
+                def _():
+                    tile_send(e, zz, yy).wait_send()
+
+        return carry
+
+    lax.fori_loop(0, QUARTERS, sent, 0)
+
+
+def fused(tables_of, query, fresh, hidden, gain, bias, keep, count, cached, weight, weight3,
+          depth, heads):
+    rows, wide = query.shape
+    head_size = HEAD_DIMENSION
+    group = wide // head_size // depth
+    contexts = depth * 4
+    quarter = rows // QUARTERS
+    half = quarter // heads
+    key_block = 512
+    cached_total = contexts * cached.shape[1]
+    fresh_total = contexts * rows
+    while cached_total % key_block or fresh_total % key_block:
+        key_block //= 2
+    pieces = EARLY + (depth - 1) * QUARTERS
+    per = depth * 2 // heads
+    model = hidden.shape[1]
+    out3 = weight3.shape[1]
+    dma = pltpu.SemaphoreType.DMA
+    bf16 = jnp.bfloat16
+    vmem = pltpu.VMEM
+    whole = pl.BlockSpec(memory_space=pltpu.VMEM)
+    far = pl.BlockSpec(memory_space=pl.ANY)
+    links = dma((QUARTERS, 2, depth))
+    return pl.pallas_call(
+        functools.partial(fused_kernel, depth, group, heads, key_block),
+        out_shape=(
+            jax.ShapeDtypeStruct(hidden.shape, bf16),
+            jax.ShapeDtypeStruct((rows, out3), bf16),
+        ),
+        in_specs=[whole] * 9 + [far] * 3,
+        out_specs=(whole, whole),
+        scratch_shapes=[
+            vmem((depth, QUARTERS, group, quarter, head_size), bf16),
+            vmem((QUARTERS, depth, group, quarter, head_size), bf16),
+            vmem((depth, 2, rows, head_size), bf16),
+            vmem((2, cached_total, head_size), bf16),
+            vmem((2, fresh_total, head_size), bf16),
+            vmem(
+                ((cached_total + fresh_total) // key_block, group * quarter, key_block),
+                jnp.float32,
+            ),
+            vmem((QUARTERS, heads, depth, 2, depth * half, group * head_size), bf16),
+            vmem((QUARTERS, depth * half, group * head_size), bf16),
+            vmem((heads, 2) + weight.shape, bf16),
+            vmem(weight3.shape, bf16),
+            vmem((rows, 2 * weight.shape[1]), jnp.float32),
+            vmem((QUARTERS, 2, depth, half, 2 * weight.shape[1]), bf16),
+            vmem((QUARTERS, heads, per, half, 2 * weight.shape[1]), bf16),
+            vmem((heads, QUARTERS, quarter, model), bf16),
+            vmem((heads, 1, model), jnp.float32),
+            dma((depth, 2)), dma((2, contexts)), dma((depth, 2)), dma((depth * 2, 2)),
+            dma((4,)), dma((QUARTERS, depth)), dma((QUARTERS, depth)),
+            dma((pieces,)), dma((pieces,)), dma((1,)), dma((1,)), dma((pieces,)), dma((pieces,)),
+            dma((QUARTERS,)), dma((QUARTERS,)),
+            links, links, links, links, links,
+            dma((QUARTERS, 2, depth)), dma((QUARTERS, heads, per)),
+            dma((QUARTERS,)), dma((QUARTERS,)), dma((1,)), dma((1,)),
+        ],
+        compiler_params=pltpu.CompilerParams(
+            collective_id=2, has_side_effects=True, vmem_limit_bytes=67043328
+        ),
+    )(*tables_of, query, fresh, hidden, gain.reshape(1, model), bias.reshape(1, out3),
+      keep.reshape(rows, 1), count.reshape(1, 1), cached, weight, weight3)
+
+
 def exchange(x, axis_name, size):
     return lax.ppermute(x, axis_name, [(i, i ^ 1) for i in range(size)])
 
@@ -371,6 +954,25 @@
     core = me % cores
     head = lax.axis_index("head")
     cosine_table, sine_table = tables(positions, head_size)
+    if heads == 2 and kv_local * 2 == chips and kv_local >= 4 and q_local == 8 * kv_local:
+        return fused(
+            (
+                jnp.concatenate([cosine_table, cosine_table], axis=1),
+                jnp.concatenate([-sine_table, sine_table], axis=1),
+            ),
+            query,
+            fresh_key_value,
+            hidden,
+            norm_gain,
+            layer3_key_value_bias,
+            keep_index,
+            keep_count,
+            cached_key_value,
+            out_weight,
+            layer3_key_value_weight,
+            kv_local,
+            heads,
+        )
     rotary_query_rows = apply_rotary(
         query.astype(jnp.float32).reshape(new_rows, q_local, head_size), cosine_table, sine_table
     ).astype(jnp.bfloat16).reshape(new_rows, q_local * head_size)

time: 463 us -> 212 us (0.46)
  the two profiles are of different devices: /device:TPU:28 before, /device:TPU:0 now
where the time goes in v2:
time: 212 us; the launch traced here: 208 us
  Pallas kernels  200 us (94%)
  local copies, waits for them, and re-layouts  5.34 us (3%)
    pallas_call x1, Pallas kernels, fused(): pl.pallas_call(functools.partial(fused_kernel, depth, group, heads, key_b...  200 us

profile of v2, /device:TPU:0, one launch (start us, length us, event | category | flops | bytes accessed | tf_op | source)
XLA Modules:
  0.0 208.0 jit_solution(13803206526320722243)
XLA Ops:
  1.3 0.7 convert_element_type.36
  2.0 1.4 copy.13.refs_7_
  3.4 0.3 fusion.2
  3.7 0.8 pad_maximum_fusion
  4.5 199.6 %shard_map.122 = (bf16[128,4096]{1,0:T(8,128)(2,1)}, bf16[128,1024]{1,0:T(8,128)(2,1)}) custom-call(f32[128,128]{1,0:T(8,128)} %get-tuple-element.8.refs_0_, f32[128,128]{1,0:T(8,128)} %get-tuple-element.9.refs_1_, bf16[128,4096]{1,0:T(8,128)(2,1)} %refs_2_.1, bf16[2,128,512]{2,1,0:T(8,128)(2,1)} %refs_3_.1, bf16[128,4096]{1,0:T(8,128)(2,1)} %refs_4_.1, ...), custom_call_target="tpu_custom_call" | custom-call | tf_op jit(solution)/shard_map/pallas_call | solution.py:886
  204.1 2.3 %copy.17 = bf16[128,4096]{1,0:T(8,128)(2,1)} copy(bf16[128,4096]{1,0:T(8,128)(2,1)} %get-tuple-element.12) | data formatting | bytes 2097152
  206.4 1.7 copy.18
  (4 shorter events, 0.0 us)
